TPU v7x, 32 devices: a whole 2x2x4 slice. The times are simulated.
32 devices in a mesh: seq: 16 (over z, y, core), grp: 2 (over x).
Axes of the slice: x: 2, y: 2, z: 4, core: 2. Of those that a mesh axis runs over, the one named last changes fastest.
Arguments:
- queries: bfloat16 [4096, 3584], P(('grp', 'seq')), parts along dimension 0, may hold values from -5 to 5
- keys: bfloat16 [4096, 512], P(('grp', 'seq')), parts along dimension 0, may hold values from -5 to 5
- values: bfloat16 [4096, 512], P(('grp', 'seq')), parts along dimension 0, may hold values from -6 to 6
- doc_lengths: int32 [16], P('grp'), parts along dimension 0, may hold values from 1 to 1280, 2048 in all
Outputs:
- attended: bfloat16 [4096, 3584], P(('grp', 'seq')), parts along dimension 0
There are 2 independent parts, one for each index of `grp`. A program takes and returns all parts, laid end to end along the dimension named above; each array names one. Nothing has to cross between parts.
Inputs may be any that keep to these rules, and one draw needn't show every extreme that they name: `doc_lengths`: the 8 documents lie one after another and their lengths sum to 2048; the longest has exactly 1280 tokens.
All inputs are finite; a program needn't handle non-finite values.
Results may differ from a plain program's by a relative error of at most 0.0085.
Values may be sent and summed in bfloat16 or wider, within the bound.
No kernel may reach another device: no remote copies, remote signals or barrier semaphores. Data moves between devices by JAX's collectives and lax.ppermute only.
A program may use at most 192 MiB of HBM per device.

v0:
```python
import jax
import jax.numpy as jnp
from jax import lax
from jax.sharding import PartitionSpec as P

HEADS = 28
KV_HEADS = 4
HEAD_DIM = 128
rope_base = 1000000.0
negative = -1e30


def doc_place(position, doc_lengths):
    doc_ends = jnp.cumsum(doc_lengths)
    beyond = position[:, None] >= doc_ends[None, :]
    doc_index = jnp.sum(beyond.astype(jnp.int32), axis=1)
    doc_start = jnp.sum(jnp.where(beyond, doc_lengths[None, :], 0), axis=1)
    return (doc_index, doc_start)


def rotate(values_in, within_doc, head_count):
    row_count = values_in.shape[0]
    half_dim = HEAD_DIM // 2
    inverse_freq = jnp.power(
        jnp.float32(rope_base), -2.0 * jnp.arange(half_dim, dtype=jnp.float32) / HEAD_DIM
    )
    angles = within_doc.astype(jnp.float32)[:, None] * inverse_freq[None, :]
    cosine = jnp.cos(angles)[:, None, :]
    sines = jnp.sin(angles)[:, None, :]
    fields = values_in.astype(jnp.float32).reshape(row_count, head_count, HEAD_DIM)
    lower_half = fields[..., :half_dim]
    upper_half = fields[..., half_dim:]
    rotated = jnp.concatenate(
        [lower_half * cosine - upper_half * sines, upper_half * cosine + lower_half * sines],
        axis=-1,
    )
    return rotated.reshape(row_count, head_count * HEAD_DIM).astype(jnp.bfloat16)


def per_device(queries, keys, values, doc_lengths):
    row_count = queries.shape[0]
    dev_index = lax.axis_index("seq")
    group_size = HEADS // KV_HEADS
    score_scale = HEAD_DIM ** (-0.5)
    local_rows = jnp.arange(row_count, dtype=jnp.int32)
    own_pos = dev_index * row_count + local_rows
    own_start = doc_place(own_pos, doc_lengths)[1]
    within_doc = own_pos - own_start
    q_rot = rotate(queries, within_doc, HEADS)
    k_rot = rotate(keys, within_doc, KV_HEADS)
    query_doc = doc_place(own_pos, doc_lengths)[0]
    q_heads = q_rot.reshape(row_count, KV_HEADS, group_size, HEAD_DIM)
    k_piece = lax.all_gather(k_rot, "seq", axis=0, tiled=True)
    v_piece = lax.all_gather(values, "seq", axis=0, tiled=True)
    length = k_piece.shape[0]
    key_pos = jnp.arange(length, dtype=jnp.int32)
    key_doc = doc_place(key_pos, doc_lengths)[0]
    allowed = (key_doc[None, :] == query_doc[:, None]) & (key_pos[None, :] <= own_pos[:, None])
    allowed_wide = allowed[:, None, None, :]
    running_max = jnp.full((row_count, KV_HEADS, group_size), negative, jnp.float32)
    k_heads = k_piece.reshape(length, KV_HEADS, HEAD_DIM)
    v_heads = v_piece.reshape(length, KV_HEADS, HEAD_DIM)
    scores = (
        jnp.einsum("qkgd,skd->qkgs", q_heads, k_heads, preferred_element_type=jnp.float32)
        * score_scale
    )
    scores = jnp.where(allowed_wide, scores, negative)
    new_max = jnp.maximum(running_max, jnp.max(scores, axis=-1))
    weight = jnp.where(allowed_wide, jnp.exp(scores - new_max[..., None]), 0.0)
    weight_sum = jnp.sum(weight, axis=-1)
    weighted = jnp.einsum(
        "qkgs,skd->qkgd", weight.astype(jnp.bfloat16), v_heads, preferred_element_type=jnp.float32
    )
    running_max, weight_sum, weighted = (new_max, weight_sum, weighted)
    attended = (
        (weighted / weight_sum[..., None]).reshape(row_count, HEADS * HEAD_DIM).astype(jnp.bfloat16)
    )
    return attended


def solution(mesh):
    return jax.shard_map(
        per_device,
        mesh=mesh,
        in_specs=(
            P(("grp", "seq"), None),
            P(("grp", "seq"), None),
            P(("grp", "seq"), None),
            P("grp"),
        ),
        out_specs=P(("grp", "seq"), None),
        check_vma=False,
    )
```

profile of v0, /device:TPU:0, one launch (start us, length us, event | category | flops | bytes accessed | tf_op | source)
XLA Modules:
  0.0 121.0 jit_solution(10799247144488770682)
XLA Ops:
  6.5 0.0 all-gather.3.cloned.1.call-start
  6.6 0.8 reduce-window.8
  7.4 0.7 fusion.10
  8.2 1.0 copy.31
  9.2 0.2 multiply_cosine_fusion
  9.4 0.7 pad_maximum_fusion.1
  10.1 0.0 all-gather.3.cloned.1.call-update
  10.1 0.0 all-gather.5.cloned.1.call-start
  10.1 0.7 all-gather.5.cloned.1.call-update
  10.9 0.1 convert_reduce_fusion
  10.9 1.6 %copy.20 = bf16[128,3584]{0,1:T(8,128)(2,1)S(1)} copy(bf16[128,3584]{1,0:T(8,128)(2,1)} %param.4) | data formatting | bytes 1835008 | tf_op args[0]
  12.5 0.2 convert.18
  12.7 0.3 fusion.9
  13.1 0.3 subtract_convert_fusion
  13.3 0.1 pad_maximum_fusion
  13.4 40.6 %all-gather.3.cloned.1.call-done = bf16[2048,512]{0,1:T(8,128)(2,1)} async-done(((bf16[128,512]{0,1:T(8,128)(2,1)}), bf16[2048,512]{0,1:T(8,128)(2,1)}) %all-gather.3.cloned.1.call-update) | async-done | bytes 2097168 | tf_op jit(solution)/shard_map/all_gather | solution.py:53
  54.0 13.3 %fusion = (f32[128,4,7]{0,2,1:T(8,128)S(1)}, f32[4,2048,128,7]{2,1,3,0:T(8,128)}) fusion(pred[128,2048]{0,1:T(8,128)(4,1)S(1)} %fusion.9, bf16[2048,4,128,1]{0,2,3,1:T(8,128)(2,1)} %bitcast.42, bf16[128,4,7,128]{0,3,2,1:T(8,128)(2,1)S(1)} %bitcast.40), kind=kOutput, calls=%fused_computation.2 | convolution fusion | flops 1901064704 | bytes 32651264 | tf_op jit(solution)/shard_map/qkgd,skd->qkgs/dot_general | solution.py:64
  67.4 13.2 %fusion.1 = f32[128,4,7]{0,2,1:T(8,128)S(1)} fusion(f32[4,2048,128,7]{2,1,3,0:T(8,128)} %get-tuple-element.14, f32[128,4,7]{0,2,1:T(8,128)S(1)} %broadcast_maximum_fusion, pred[128,2048]{0,1:T(8,128)(4,1)S(1)} %fusion.9), kind=kLoop, calls=%fused_computation.3 | loop fusion | flops 36696576 | bytes 29650944 | tf_op jit(solution)/shard_map/reduce_sum | solution.py:70
  80.6 16.2 %all-gather.5.cloned.1.call-done = bf16[2048,512]{1,0:T(8,128)(2,1)} async-done(((bf16[128,512]{1,0:T(8,128)(2,1)}), bf16[2048,512]{1,0:T(8,128)(2,1)}) %all-gather.5.cloned.1.call-update) | async-done | bytes 2097168 | tf_op jit(solution)/shard_map/all_gather | solution.py:54
  96.8 2.9 %copy.23 = bf16[2048,512]{0,1:T(8,128)(2,1)S(1)} copy(bf16[2048,512]{1,0:T(8,128)(2,1)} %all-gather.5.cloned.1.call-done) | data formatting | bytes 4194304 | tf_op jit(solution)/shard_map/all_gather | solution.py:54
  99.7 13.2 %fusion.6 = bf16[128,4,7,128]{0,3,2,1:T(8,128)(2,1)S(1)} fusion(bf16[2048,4,128,1]{0,2,3,1:T(8,128)(2,1)S(1)} %bitcast.41, f32[4,2048,128,7]{2,1,3,0:T(8,128)} %get-tuple-element.14, f32[128,4,7]{0,2,1:T(8,128)S(1)} %broadcast_maximum_fusion, pred[128,2048]{0,1:T(8,128)(4,1)S(1)} %fusion.9, f32[128,4,7]{0,2,1:T(8,128)S(1)} %fusion.1), kind=kOutput, calls=%fused_computation.8 | convolution fusion | flops 1916665856 | bytes 32665600 | tf_op jit(solution)/shard_map/qkgs,skd->qkgd/dot_general | solution.py:71
  112.9 1.3 %copy.25 = bf16[128,3584]{1,0:T(8,128)(2,1)} copy(bf16[128,3584]{0,1:T(8,128)(2,1)S(1)} %bitcast.44) | data formatting | bytes 1835008 | tf_op jit(solution)/shard_map/convert_element_type | solution.py:76
  (5 shorter events, 0.1 us)
Async XLA Ops:
  6.5 47.5 %all-gather.3.cloned.1.call-start = ((), (), s32[]{:S(2)}) async-start(), calls=%async_computation | async-start | bytes 2228224 | tf_op jit(solution)/shard_map/all_gather | solution.py:53
  10.1 86.7 %all-gather.5.cloned.1.call-start = ((), (), s32[]{:S(2)}) async-start(), calls=%async_computation.1 | async-start | bytes 2228224 | tf_op jit(solution)/shard_map/all_gather | solution.py:54
Sparse Core Ops, SparseCore 0:
  10.2 43.7 all-gather.2
  56.2 40.5 all-gather.4
where the time goes:
time: 121 us
  waiting for transfers between devices  57.5 us (48%)
  matrix products  26.5 us (22%)
  other arithmetic  16.7 us (14%)
  between operations  13.5 us (11%)
  local copies, waits for them, and re-layouts  6.76 us (6%)
    all_gather x1, waiting for transfers between devices, per_device(): k_piece = lax.all_gather(k_rot, 'seq', axis=0, tiled=True)  40.6 us
    all_gather x1, waiting for transfers between devices, per_device(): v_piece = lax.all_gather(values, 'seq', axis=0, tiled=True)  16.2 us
    dot_general x1, matrix products, per_device(): jnp.einsum('qkgd,skd->qkgs', q_heads, k_heads, preferred_element_type=jnp...  13.3 us
    reduce_sum x1, other arithmetic, per_device(): weight_sum = jnp.sum(weight, axis=-1)  13.2 us
    dot_general x1, matrix products, per_device(): jnp.einsum('qkgs,skd->qkgd', weight.astype(jnp.bfloat16), v_heads, prefer...  13.2 us
    all_gather x1, local copies, waits for them, and re-layouts, per_device(): v_piece = lax.all_gather(values, 'seq', axis=0, tiled=True)  2.93 us
  transfers between devices with their start and end apart: 2, of which 2 were waited for; matrix products, arithmetic and copies ran while one was open for 24% of the time, Pallas kernels for 0%

commit v1 on v0

--- a/solution.py
+++ b/solution.py
@@ -51,7 +51,13 @@
     query_doc = doc_place(own_pos, doc_lengths)[0]
     q_heads = q_rot.reshape(row_count, KV_HEADS, group_size, HEAD_DIM)
     k_piece = lax.all_gather(k_rot, "seq", axis=0, tiled=True)
-    v_piece = lax.all_gather(values, "seq", axis=0, tiled=True)
+    n_dev = lax.axis_size("seq")
+    held, pieces = (values, [values])
+    for _ in range(n_dev - 1):
+        held = lax.ppermute(held, "seq", [(i, (i + 1) % n_dev) for i in range(n_dev)])
+        pieces.insert(0, held)
+    line = jnp.concatenate(pieces, axis=0)
+    v_piece = jnp.roll(line, (lax.axis_index("seq") + 1) * values.shape[0], axis=0)
     length = k_piece.shape[0]
     key_pos = jnp.arange(length, dtype=jnp.int32)
     key_doc = doc_place(key_pos, doc_lengths)[0]

time: 121 us -> 178 us (1.47)
  waiting for transfers between devices: 57.5 us -> 108 us
  local copies, waits for them, and re-layouts: 6.76 us -> 11.4 us
    ppermute x0 -> x15, waiting for transfers between devices: none -> 102 us  [per_device(): lax.ppermute(held, 'seq', [(i, (i + 1) % n_dev) for i in range(n_dev)])]
    all_gather x1, waiting for transfers between devices: 40.6 us -> 5.97 us  [per_device(): k_piece = lax.all_gather(k_rot, 'seq', axis=0, tiled=True)]
    all_gather x1 -> x0, waiting for transfers between devices: 16.2 us -> none  [per_device(): v_piece = lax.all_gather(values, 'seq', axis=0, tiled=True)]
    unnamed x1 -> x48, local copies, waits for them, and re-layouts: 1.55 us -> 6.45 us
    all_gather x1 -> x0, local copies, waits for them, and re-layouts: 2.93 us -> none  [per_device(): v_piece = lax.all_gather(values, 'seq', axis=0, tiled=True)]
    dynamic_slice x0 -> x2, local copies, waits for them, and re-layouts: none -> 2.63 us  [per_device(): jnp.roll(line, (lax.axis_index('seq') + 1) * values.shape[0], axis=0)]
  transfers between devices with their start and end apart: 2 -> 16, of which waited for: 2 -> 16; matrix products, arithmetic and copies ran while one was open for 24% -> 8% of each run, Pallas kernels for 0% -> 0%
where the time goes in v1:
time: 178 us; the launch traced here: 177 us
  waiting for transfers between devices  108 us (61%)
  matrix products  26.3 us (15%)
  other arithmetic  16.8 us (9%)
  between operations  13.8 us (8%)
  local copies, waits for them, and re-layouts  11.4 us (6%)
    ppermute x15, waiting for transfers between devices, per_device(): lax.ppermute(held, 'seq', [(i, (i + 1) % n_dev) for i in range(n_dev)])  102 us
    reduce_sum x1, other arithmetic, per_device(): weight_sum = jnp.sum(weight, axis=-1)  13.3 us
    dot_general x1, matrix products, per_device(): jnp.einsum('qkgs,skd->qkgd', weight.astype(jnp.bfloat16), v_heads, prefer...  13.2 us
    dot_general x1, matrix products, per_device(): jnp.einsum('qkgd,skd->qkgs', q_heads, k_heads, preferred_element_type=jnp...  13.1 us
    unnamed x48, local copies, waits for them, and re-layouts  6.45 us
    all_gather x1, waiting for transfers between devices, per_device(): k_piece = lax.all_gather(k_rot, 'seq', axis=0, tiled=True)  5.97 us
  transfers between devices with their start and end apart: 16, of which 16 were waited for; matrix products, arithmetic and copies ran while one was open for 8% of the time, Pallas kernels for 0%

profile of v1, /device:TPU:0, one launch (start us, length us, event | category | flops | bytes accessed | tf_op | source)
XLA Modules:
  0.0 177.2 jit_solution(17972475519825413711)
XLA Ops:
  6.5 0.0 all-gather.2.cloned.1.call-start
  6.5 0.5 collective-permute-start
  7.0 7.8 %collective-permute-done = bf16[128,512]{1,0:T(8,128)(2,1)S(1)} collective-permute-done((bf16[128,512]{1,0:T(8,128)(2,1)}, bf16[128,512]{1,0:T(8,128)(2,1)S(1)}, u32[]{:S(2)}, u32[]{:S(2)}) %collective-permute-start) | collective-permute-done | bytes 131104 | tf_op jit(solution)/shard_map/ppermute | solution.py:57
  14.9 0.0 collective-permute-start.1
  14.9 7.1 %collective-permute-done.1 = bf16[128,512]{1,0:T(8,128)(2,1)S(1)} collective-permute-done((bf16[128,512]{1,0:T(8,128)(2,1)S(1)}, bf16[128,512]{1,0:T(8,128)(2,1)S(1)}, u32[]{:S(2)}, u32[]{:S(2)}) %collective-permute-start.1) | collective-permute-done | bytes 131104 | tf_op jit(solution)/shard_map/ppermute | solution.py:57
  22.0 0.0 collective-permute-start.2
  22.0 7.1 %collective-permute-done.2 = bf16[128,512]{1,0:T(8,128)(2,1)S(1)} collective-permute-done((bf16[128,512]{1,0:T(8,128)(2,1)S(1)}, bf16[128,512]{1,0:T(8,128)(2,1)S(1)}, u32[]{:S(2)}, u32[]{:S(2)}) %collective-permute-start.2) | collective-permute-done | bytes 131104 | tf_op jit(solution)/shard_map/ppermute | solution.py:57
  29.1 0.0 collective-permute-start.3
  29.1 7.1 %collective-permute-done.3 = bf16[128,512]{1,0:T(8,128)(2,1)S(1)} collective-permute-done((bf16[128,512]{1,0:T(8,128)(2,1)S(1)}, bf16[128,512]{1,0:T(8,128)(2,1)S(1)}, u32[]{:S(2)}, u32[]{:S(2)}) %collective-permute-start.3) | collective-permute-done | bytes 131104 | tf_op jit(solution)/shard_map/ppermute | solution.py:57
  36.1 0.0 collective-permute-start.4
  36.1 7.1 %collective-permute-done.4 = bf16[128,512]{1,0:T(8,128)(2,1)S(1)} collective-permute-done((bf16[128,512]{1,0:T(8,128)(2,1)S(1)}, bf16[128,512]{1,0:T(8,128)(2,1)S(1)}, u32[]{:S(2)}, u32[]{:S(2)}) %collective-permute-start.4) | collective-permute-done | bytes 131104 | tf_op jit(solution)/shard_map/ppermute | solution.py:57
  43.2 0.0 collective-permute-start.5
  43.2 7.1 %collective-permute-done.5 = bf16[128,512]{1,0:T(8,128)(2,1)S(1)} collective-permute-done((bf16[128,512]{1,0:T(8,128)(2,1)S(1)}, bf16[128,512]{1,0:T(8,128)(2,1)S(1)}, u32[]{:S(2)}, u32[]{:S(2)}) %collective-permute-start.5) | collective-permute-done | bytes 131104 | tf_op jit(solution)/shard_map/ppermute | solution.py:57
  50.3 0.0 collective-permute-start.6
  50.3 7.1 %collective-permute-done.6 = bf16[128,512]{1,0:T(8,128)(2,1)S(1)} collective-permute-done((bf16[128,512]{1,0:T(8,128)(2,1)S(1)}, bf16[128,512]{1,0:T(8,128)(2,1)S(1)}, u32[]{:S(2)}, u32[]{:S(2)}) %collective-permute-start.6) | collective-permute-done | bytes 131104 | tf_op jit(solution)/shard_map/ppermute | solution.py:57
  57.4 0.0 collective-permute-start.7
  57.4 0.8 reduce-window.8
  58.3 0.7 fusion.10
  59.0 5.5 %collective-permute-done.7 = bf16[128,512]{1,0:T(8,128)(2,1)S(1)} collective-permute-done((bf16[128,512]{1,0:T(8,128)(2,1)S(1)}, bf16[128,512]{1,0:T(8,128)(2,1)S(1)}, u32[]{:S(2)}, u32[]{:S(2)}) %collective-permute-start.7) | collective-permute-done | bytes 131104 | tf_op jit(solution)/shard_map/ppermute | solution.py:57
  64.5 0.0 collective-permute-start.8
  64.5 1.0 copy.31
  65.5 6.1 %collective-permute-done.8 = bf16[128,512]{1,0:T(8,128)(2,1)S(1)} collective-permute-done((bf16[128,512]{1,0:T(8,128)(2,1)S(1)}, bf16[128,512]{1,0:T(8,128)(2,1)S(1)}, u32[]{:S(2)}, u32[]{:S(2)}) %collective-permute-start.8) | collective-permute-done | bytes 131104 | tf_op jit(solution)/shard_map/ppermute | solution.py:57
  71.6 0.0 collective-permute-start.9
  71.6 0.2 multiply_cosine_fusion
  71.8 6.9 %collective-permute-done.9 = bf16[128,512]{1,0:T(8,128)(2,1)S(1)} collective-permute-done((bf16[128,512]{1,0:T(8,128)(2,1)S(1)}, bf16[128,512]{1,0:T(8,128)(2,1)S(1)}, u32[]{:S(2)}, u32[]{:S(2)}) %collective-permute-start.9) | collective-permute-done | bytes 131104 | tf_op jit(solution)/shard_map/ppermute | solution.py:57
  78.7 0.0 collective-permute-start.10
  78.7 7.0 %collective-permute-done.10 = bf16[128,512]{1,0:T(8,128)(2,1)S(1)} collective-permute-done((bf16[128,512]{1,0:T(8,128)(2,1)S(1)}, bf16[128,512]{1,0:T(8,128)(2,1)S(1)}, u32[]{:S(2)}, u32[]{:S(2)}) %collective-permute-start.10) | collective-permute-done | bytes 131104 | tf_op jit(solution)/shard_map/ppermute | solution.py:57
  85.8 0.0 collective-permute-start.11
  85.8 0.7 pad_maximum_fusion.1
  86.5 0.0 all-gather.2.cloned.1.call-update
  86.5 0.1 convert_reduce_fusion
  86.6 6.3 %collective-permute-done.11 = bf16[128,512]{1,0:T(8,128)(2,1)S(1)} collective-permute-done((bf16[128,512]{1,0:T(8,128)(2,1)S(1)}, bf16[128,512]{1,0:T(8,128)(2,1)S(1)}, u32[]{:S(2)}, u32[]{:S(2)}) %collective-permute-start.11) | collective-permute-done | bytes 131104 | tf_op jit(solution)/shard_map/ppermute | solution.py:57
  92.9 0.0 collective-permute-start.12
  92.9 0.3 fusion.9
  93.2 1.6 copy.21
  94.8 0.2 convert.18
  95.0 0.0 copy-start.1
  95.0 5.1 %collective-permute-done.12 = bf16[128,512]{1,0:T(8,128)(2,1)S(1)} collective-permute-done((bf16[128,512]{1,0:T(8,128)(2,1)S(1)}, bf16[128,512]{1,0:T(8,128)(2,1)S(1)}, u32[]{:S(2)}, u32[]{:S(2)}) %collective-permute-start.12) | collective-permute-done | bytes 131104 | tf_op jit(solution)/shard_map/ppermute | solution.py:57
  100.1 0.0 collective-permute-start.13
  100.1 0.3 subtract_convert_fusion
  100.4 8.0 %collective-permute-done.13 = bf16[128,512]{1,0:T(8,128)(2,1)} collective-permute-done((bf16[128,512]{1,0:T(8,128)(2,1)S(1)}, bf16[128,512]{1,0:T(8,128)(2,1)}, u32[]{:S(2)}, u32[]{:S(2)}) %collective-permute-start.13) | collective-permute-done | bytes 131104 | tf_op jit(solution)/shard_map/ppermute | solution.py:57
  108.3 0.0 collective-permute-start.14
  108.3 0.0 copy-done.2
  108.3 0.0 copy-done.4
  108.3 0.0 copy-done.6
  108.3 0.0 copy-start.7
  108.4 0.0 copy-start.5
  108.4 0.0 copy-start.3
  108.4 0.1 pad_maximum_fusion
  108.4 7.2 %collective-permute-done.14 = bf16[128,512]{1,0:T(8,128)(2,1)S(1)} collective-permute-done((bf16[128,512]{1,0:T(8,128)(2,1)}, bf16[128,512]{1,0:T(8,128)(2,1)S(1)}, u32[]{:S(2)}, u32[]{:S(2)}) %collective-permute-start.14) | collective-permute-done | bytes 131104 | tf_op jit(solution)/shard_map/ppermute | solution.py:57
  115.7 0.9 constant_dynamic-update-slice_fusion.30
  116.6 0.9 constant_dynamic-update-slice_fusion.29
  117.5 0.9 constant_dynamic-update-slice_fusion.28
  118.4 0.9 constant_dynamic-update-slice_fusion.27
  119.5 0.0 copy-done.1
  119.6 0.9 constant_dynamic-update-slice_fusion.14
  120.8 0.1 constant_dynamic-slice_fusion
  120.9 2.5 %copy.18 = bf16[2048,512]{0,1:T(8,128)(2,1)} copy(bf16[2048,512]{1,0:T(8,128)(2,1)S(1)} %constant_dynamic-slice_fusion) | data formatting | bytes 4194304 | tf_op jit(solution)/shard_map/jit(_roll_dynamic)/dynamic_slice | solution.py:60
  123.4 6.0 %all-gather.2.cloned.1.call-done = bf16[2048,512]{0,1:T(8,128)(2,1)} async-done(((bf16[128,512]{0,1:T(8,128)(2,1)}), bf16[2048,512]{0,1:T(8,128)(2,1)}) %all-gather.2.cloned.1.call-update) | async-done | bytes 2097168 | tf_op jit(solution)/shard_map/all_gather | solution.py:53
  129.4 13.1 %fusion = (f32[128,4,7]{0,2,1:T(8,128)S(1)}, f32[4,2048,128,7]{2,1,3,0:T(8,128)}) fusion(pred[128,2048]{0,1:T(8,128)(4,1)S(1)} %fusion.9, bf16[2048,4,128,1]{0,2,3,1:T(8,128)(2,1)} %bitcast.42, bf16[128,4,7,128]{0,3,2,1:T(8,128)(2,1)S(1)} %bitcast.40), kind=kOutput, calls=%fused_computation.2 | convolution fusion | flops 1901064704 | bytes 32651264 | tf_op jit(solution)/shard_map/qkgd,skd->qkgs/dot_general | solution.py:70
  142.5 13.3 %fusion.1 = f32[128,4,7]{0,2,1:T(8,128)S(1)} fusion(f32[4,2048,128,7]{2,1,3,0:T(8,128)} %get-tuple-element.14, f32[128,4,7]{0,2,1:T(8,128)S(1)} %broadcast_maximum_fusion, pred[128,2048]{0,1:T(8,128)(4,1)S(1)} %fusion.9), kind=kLoop, calls=%fused_computation.3 | loop fusion | flops 36696576 | bytes 29650944 | tf_op jit(solution)/shard_map/reduce_sum | solution.py:76
  155.8 0.0 copy-done
  155.8 13.2 %fusion.6 = bf16[128,4,7,128]{0,3,2,1:T(8,128)(2,1)S(1)} fusion(bf16[2048,4,128,1]{0,2,3,1:T(8,128)(2,1)S(1)} %bitcast.41, f32[4,2048,128,7]{2,1,3,0:T(8,128)} %get-tuple-element.14, f32[128,4,7]{0,2,1:T(8,128)S(1)} %broadcast_maximum_fusion, pred[128,2048]{0,1:T(8,128)(4,1)S(1)} %fusion.9, f32[128,4,7]{0,2,1:T(8,128)S(1)} %fusion.1), kind=kOutput, calls=%fused_computation.8 | convolution fusion | flops 1916665856 | bytes 32665600 | tf_op jit(solution)/shard_map/qkgs,skd->qkgd/dot_general | solution.py:77
  169.0 1.3 copy.25
  (39 shorter events, 0.4 us)
Async XLA Ops:
  6.5 122.9 %all-gather.2.cloned.1.call-start = ((), (), s32[]{:S(2)}) async-start(), calls=%async_computation | async-start | bytes 2228224 | tf_op jit(solution)/shard_map/all_gather | solution.py:53
  6.5 8.3 %collective-permute-start = (bf16[128,512]{1,0:T(8,128)(2,1)}, bf16[128,512]{1,0:T(8,128)(2,1)S(1)}, u32[]{:S(2)}, u32[]{:S(2)}) collective-permute-start(bf16[128,512]{1,0:T(8,128)(2,1)} %param.6), channel_id=1, source_target_pairs={{0,2},{2,4},{4,6},{6,8},{8,10},{10,12},{12,14},{14,16},{16,18},{18... | collective-permute-start | bytes 393224 | tf_op jit(solution)/shard_map/ppermute | solution.py:57
  14.9 7.1 %collective-permute-start.1 = (bf16[128,512]{1,0:T(8,128)(2,1)S(1)}, bf16[128,512]{1,0:T(8,128)(2,1)S(1)}, u32[]{:S(2)}, u32[]{:S(2)}) collective-permute-start(bf16[128,512]{1,0:T(8,128)(2,1)S(1)} %collective-permute-done), channel_id=1, source_target_pairs={{0,2},{2,4},{4,6},{6,8},{8,10},{10,12},{12,14},{14,16},{16,18},{18... | collective-permute-start | bytes 393224 | tf_op jit(solution)/shard_map/ppermute | solution.py:57
  22.0 7.1 %collective-permute-start.2 = (bf16[128,512]{1,0:T(8,128)(2,1)S(1)}, bf16[128,512]{1,0:T(8,128)(2,1)S(1)}, u32[]{:S(2)}, u32[]{:S(2)}) collective-permute-start(bf16[128,512]{1,0:T(8,128)(2,1)S(1)} %collective-permute-done.1), channel_id=1, source_target_pairs={{0,2},{2,4},{4,6},{6,8},{8,10},{10,12},{12,14},{14,16},{16,18},{18... | collective-permute-start | bytes 393224 | tf_op jit(solution)/shard_map/ppermute | solution.py:57
  29.1 7.1 %collective-permute-start.3 = (bf16[128,512]{1,0:T(8,128)(2,1)S(1)}, bf16[128,512]{1,0:T(8,128)(2,1)S(1)}, u32[]{:S(2)}, u32[]{:S(2)}) collective-permute-start(bf16[128,512]{1,0:T(8,128)(2,1)S(1)} %collective-permute-done.2), channel_id=1, source_target_pairs={{0,2},{2,4},{4,6},{6,8},{8,10},{10,12},{12,14},{14,16},{16,18},{18... | collective-permute-start | bytes 393224 | tf_op jit(solution)/shard_map/ppermute | solution.py:57
  36.1 7.1 %collective-permute-start.4 = (bf16[128,512]{1,0:T(8,128)(2,1)S(1)}, bf16[128,512]{1,0:T(8,128)(2,1)S(1)}, u32[]{:S(2)}, u32[]{:S(2)}) collective-permute-start(bf16[128,512]{1,0:T(8,128)(2,1)S(1)} %collective-permute-done.3), channel_id=1, source_target_pairs={{0,2},{2,4},{4,6},{6,8},{8,10},{10,12},{12,14},{14,16},{16,18},{18... | collective-permute-start | bytes 393224 | tf_op jit(solution)/shard_map/ppermute | solution.py:57
  43.2 7.1 %collective-permute-start.5 = (bf16[128,512]{1,0:T(8,128)(2,1)S(1)}, bf16[128,512]{1,0:T(8,128)(2,1)S(1)}, u32[]{:S(2)}, u32[]{:S(2)}) collective-permute-start(bf16[128,512]{1,0:T(8,128)(2,1)S(1)} %collective-permute-done.4), channel_id=1, source_target_pairs={{0,2},{2,4},{4,6},{6,8},{8,10},{10,12},{12,14},{14,16},{16,18},{18... | collective-permute-start | bytes 393224 | tf_op jit(solution)/shard_map/ppermute | solution.py:57
  50.3 7.1 %collective-permute-start.6 = (bf16[128,512]{1,0:T(8,128)(2,1)S(1)}, bf16[128,512]{1,0:T(8,128)(2,1)S(1)}, u32[]{:S(2)}, u32[]{:S(2)}) collective-permute-start(bf16[128,512]{1,0:T(8,128)(2,1)S(1)} %collective-permute-done.5), channel_id=1, source_target_pairs={{0,2},{2,4},{4,6},{6,8},{8,10},{10,12},{12,14},{14,16},{16,18},{18... | collective-permute-start | bytes 393224 | tf_op jit(solution)/shard_map/ppermute | solution.py:57
  57.4 7.1 %collective-permute-start.7 = (bf16[128,512]{1,0:T(8,128)(2,1)S(1)}, bf16[128,512]{1,0:T(8,128)(2,1)S(1)}, u32[]{:S(2)}, u32[]{:S(2)}) collective-permute-start(bf16[128,512]{1,0:T(8,128)(2,1)S(1)} %collective-permute-done.6), channel_id=1, source_target_pairs={{0,2},{2,4},{4,6},{6,8},{8,10},{10,12},{12,14},{14,16},{16,18},{18... | collective-permute-start | bytes 393224 | tf_op jit(solution)/shard_map/ppermute | solution.py:57
  64.5 7.1 %collective-permute-start.8 = (bf16[128,512]{1,0:T(8,128)(2,1)S(1)}, bf16[128,512]{1,0:T(8,128)(2,1)S(1)}, u32[]{:S(2)}, u32[]{:S(2)}) collective-permute-start(bf16[128,512]{1,0:T(8,128)(2,1)S(1)} %collective-permute-done.7), channel_id=1, source_target_pairs={{0,2},{2,4},{4,6},{6,8},{8,10},{10,12},{12,14},{14,16},{16,18},{18... | collective-permute-start | bytes 393224 | tf_op jit(solution)/shard_map/ppermute | solution.py:57
  71.6 7.1 %collective-permute-start.9 = (bf16[128,512]{1,0:T(8,128)(2,1)S(1)}, bf16[128,512]{1,0:T(8,128)(2,1)S(1)}, u32[]{:S(2)}, u32[]{:S(2)}) collective-permute-start(bf16[128,512]{1,0:T(8,128)(2,1)S(1)} %collective-permute-done.8), channel_id=1, source_target_pairs={{0,2},{2,4},{4,6},{6,8},{8,10},{10,12},{12,14},{14,16},{16,18},{18... | collective-permute-start | bytes 393224 | tf_op jit(solution)/shard_map/ppermute | solution.py:57
  78.7 7.1 %collective-permute-start.10 = (bf16[128,512]{1,0:T(8,128)(2,1)S(1)}, bf16[128,512]{1,0:T(8,128)(2,1)S(1)}, u32[]{:S(2)}, u32[]{:S(2)}) collective-permute-start(bf16[128,512]{1,0:T(8,128)(2,1)S(1)} %collective-permute-done.9), channel_id=1, source_target_pairs={{0,2},{2,4},{4,6},{6,8},{8,10},{10,12},{12,14},{14,16},{16,18},{18... | collective-permute-start | bytes 393224 | tf_op jit(solution)/shard_map/ppermute | solution.py:57
  85.8 22.5 %copy-start.2 = (bf16[128,512]{1,0:T(8,128)(2,1)}, bf16[128,512]{1,0:T(8,128)(2,1)S(1)}, u32[]{:S(2)}) copy-start(bf16[128,512]{1,0:T(8,128)(2,1)S(1)} %collective-permute-done.10) | copy-start | bytes 393220
  85.8 7.1 %collective-permute-start.11 = (bf16[128,512]{1,0:T(8,128)(2,1)S(1)}, bf16[128,512]{1,0:T(8,128)(2,1)S(1)}, u32[]{:S(2)}, u32[]{:S(2)}) collective-permute-start(bf16[128,512]{1,0:T(8,128)(2,1)S(1)} %collective-permute-done.10), channel_id=1, source_target_pairs={{0,2},{2,4},{4,6},{6,8},{8,10},{10,12},{12,14},{14,16},{16,18},{18... | collective-permute-start | bytes 393224 | tf_op jit(solution)/shard_map/ppermute | solution.py:57
  92.9 15.5 %copy-start.4 = (bf16[128,512]{1,0:T(8,128)(2,1)}, bf16[128,512]{1,0:T(8,128)(2,1)S(1)}, u32[]{:S(2)}) copy-start(bf16[128,512]{1,0:T(8,128)(2,1)S(1)} %collective-permute-done.11) | copy-start | bytes 393220
  92.9 7.2 %collective-permute-start.12 = (bf16[128,512]{1,0:T(8,128)(2,1)S(1)}, bf16[128,512]{1,0:T(8,128)(2,1)S(1)}, u32[]{:S(2)}, u32[]{:S(2)}) collective-permute-start(bf16[128,512]{1,0:T(8,128)(2,1)S(1)} %collective-permute-done.11), channel_id=1, source_target_pairs={{0,2},{2,4},{4,6},{6,8},{8,10},{10,12},{12,14},{14,16},{16,18},{18... | collective-permute-start | bytes 393224 | tf_op jit(solution)/shard_map/ppermute | solution.py:57
  95.0 24.6 %copy-start.1 = (bf16[128,512]{1,0:T(8,128)(2,1)S(1)}, bf16[128,512]{1,0:T(8,128)(2,1)}, u32[]{:S(2)}) copy-start(bf16[128,512]{1,0:T(8,128)(2,1)} %param.6) | copy-start | bytes 393220
  100.1 8.3 %copy-start.6 = (bf16[128,512]{1,0:T(8,128)(2,1)}, bf16[128,512]{1,0:T(8,128)(2,1)S(1)}, u32[]{:S(2)}) copy-start(bf16[128,512]{1,0:T(8,128)(2,1)S(1)} %collective-permute-done.12) | copy-start | bytes 393220
  100.1 8.3 %collective-permute-start.13 = (bf16[128,512]{1,0:T(8,128)(2,1)S(1)}, bf16[128,512]{1,0:T(8,128)(2,1)}, u32[]{:S(2)}, u32[]{:S(2)}) collective-permute-start(bf16[128,512]{1,0:T(8,128)(2,1)S(1)} %collective-permute-done.12), channel_id=1, source_target_pairs={{0,2},{2,4},{4,6},{6,8},{8,10},{10,12},{12,14},{14,16},{16,18},{18... | collective-permute-start | bytes 393224 | tf_op jit(solution)/shard_map/ppermute | solution.py:57
  108.3 7.3 %collective-permute-start.14 = (bf16[128,512]{1,0:T(8,128)(2,1)}, bf16[128,512]{1,0:T(8,128)(2,1)S(1)}, u32[]{:S(2)}, u32[]{:S(2)}) collective-permute-start(bf16[128,512]{1,0:T(8,128)(2,1)} %collective-permute-done.13), channel_id=1, source_target_pairs={{0,2},{2,4},{4,6},{6,8},{8,10},{10,12},{12,14},{14,16},{16,18},{18... | collective-permute-start | bytes 393224 | tf_op jit(solution)/shard_map/ppermute | solution.py:57
  108.3 12.2 %copy-start.7 = (bf16[128,512]{1,0:T(8,128)(2,1)S(1)}, bf16[128,512]{1,0:T(8,128)(2,1)}, u32[]{:S(2)}) copy-start(bf16[128,512]{1,0:T(8,128)(2,1)} %copy-done.6) | copy-start | bytes 393220
  108.4 12.2 %copy-start.5 = (bf16[128,512]{1,0:T(8,128)(2,1)S(1)}, bf16[128,512]{1,0:T(8,128)(2,1)}, u32[]{:S(2)}) copy-start(bf16[128,512]{1,0:T(8,128)(2,1)} %copy-done.4) | copy-start | bytes 393220
  108.4 12.2 %copy-start.3 = (bf16[128,512]{1,0:T(8,128)(2,1)S(1)}, bf16[128,512]{1,0:T(8,128)(2,1)}, u32[]{:S(2)}) copy-start(bf16[128,512]{1,0:T(8,128)(2,1)} %copy-done.2) | copy-start | bytes 393220
  142.5 13.3 %copy-start = (bf16[2048,512]{0,1:T(8,128)(2,1)S(1)}, bf16[2048,512]{0,1:T(8,128)(2,1)}, u32[]{:S(2)}) copy-start(bf16[2048,512]{0,1:T(8,128)(2,1)} %copy.18) | copy-start | bytes 6291460
Sparse Core Ops, SparseCore 0:
  86.6 42.7 all-gather.1
